TPU v7x, 32 devices: a whole 2x2x4 slice. The times are simulated.
32 devices in a mesh: dp: 8 (over z, core), tp: 4 (over y, x).
Axes of the slice: x: 2, y: 2, z: 4, core: 2. Of those that a mesh axis runs over, the one named last changes fastest.
Arguments:
- tokens: bfloat16 [4096, 4096], P('dp'), may hold values from -6 to 6
- gain: float32 [4096], replicated, may hold values from 0.1 to 1.9
- router: float32 [4096, 8], replicated, may hold values from -0.09375 to 0.09375
- routes: int32 [4096, 2], P('dp'), may hold values from 0 to 7, all different within a row
- w_gate: bfloat16 [2, 4096, 1024], P(None, 'dp', 'tp'), may hold values from -0.125 to 0.125
- w_up: bfloat16 [2, 4096, 1024], P(None, 'dp', 'tp'), may hold values from -0.125 to 0.125
- w_down: bfloat16 [2, 1024, 4096], P(None, 'dp', 'tp'), may hold values from -0.25 to 0.25
Outputs:
- mixed: bfloat16 [4096, 4096], P('dp', 'tp')
Inputs may be any that keep to these rules, and one draw needn't show every extreme that they name: `routes`: each row names two different experts.
All inputs are finite; a program needn't handle non-finite values.
Results may differ from a plain program's by a relative error of at most 0.0065.
Values may be sent and summed in bfloat16 or wider, within the bound.
A program may use at most 64 MiB of HBM per device.

v0:
```python
import jax
import jax.numpy as jnp
from jax import lax
from jax.sharding import PartitionSpec as P

EPS = 1e-06
ROUTE_SCALE = 2.5


def per_device(tokens, gain, router, routes, w_gate, w_up, w_down):
    values = tokens.astype(jnp.float32)
    square = jnp.mean(values * values, axis=-1, keepdims=True)
    normed = (values * lax.rsqrt(square + EPS) * gain).astype(jnp.bfloat16)
    scores = jax.nn.sigmoid(
        jnp.dot(normed.astype(jnp.float32), router, precision=lax.Precision.HIGHEST)
    )
    labels = jnp.arange(router.shape[1], dtype=jnp.int32)
    picked_mask = (routes[:, :, None] == labels[None, None, :]).astype(jnp.float32)
    picked = jnp.sum(picked_mask * scores[:, None, :], axis=-1)
    chosen = jnp.sum(picked_mask, axis=1)
    combine = chosen * scores * ROUTE_SCALE / jnp.sum(picked, axis=-1, keepdims=True)
    held_weights = combine[:, : w_gate.shape[0]]
    full_gate, full_up, full_down = (
        lax.all_gather(w_gate, "dp", axis=1, tiled=True),
        lax.all_gather(w_up, "dp", axis=1, tiled=True),
        lax.all_gather(w_down, "dp", axis=1, tiled=True),
    )
    gate_value = jnp.einsum("td,edf->tef", normed, full_gate, preferred_element_type=jnp.float32)
    up_value = jnp.einsum("td,edf->tef", normed, full_up, preferred_element_type=jnp.float32)
    hidden = (jax.nn.silu(gate_value) * up_value * held_weights[:, :, None]).astype(jnp.bfloat16)
    whole_hidden = lax.all_gather(hidden, "tp", axis=2, tiled=True)
    mixed = jnp.einsum("tef,efd->td", whole_hidden, full_down, preferred_element_type=jnp.float32)
    return mixed.astype(jnp.bfloat16)


def solution(mesh):
    return jax.shard_map(
        per_device,
        mesh=mesh,
        in_specs=(
            P("dp", None),
            P(),
            P(),
            P("dp", None),
            P(None, "dp", "tp"),
            P(None, "dp", "tp"),
            P(None, "dp", "tp"),
        ),
        out_specs=P("dp", "tp"),
        check_vma=False,
    )
```

profile of v0, /device:TPU:0, one launch (start us, length us, event | category | flops | bytes accessed | tf_op | source)
XLA Modules:
  0.0 201.4 jit_solution(2412415738272658088)
XLA Ops:
  6.5 0.0 copy-start
  6.5 0.0 copy-start.3
  6.5 0.0 all-gather.5.cloned.1.call-start
  6.5 0.7 all-gather.5.cloned.1.call-update
  7.3 0.0 all-gather.7.cloned.1.call-start
  7.3 0.7 all-gather.7.cloned.1.call-update
  8.0 0.0 all-gather.11.cloned.1.call-start
  8.1 0.7 all-gather.11.cloned.1.call-update
  8.7 0.0 all-gather.9.cloned.1.call-start
  8.8 0.0 copy-start.1
  8.8 3.2 %fusion = f32[512]{0:T(512)S(1)} fusion(bf16[512,4096]{1,0:T(8,128)(2,1)} %param.7), kind=kLoop, calls=%fused_computation.2 | loop fusion | flops 6290944 | bytes 4196352 | tf_op jit(solution)/shard_map/reduce_sum | solution.py:12
  12.0 0.0 copy-start.2
  12.1 0.0 copy-done
  12.1 0.0 copy-done.3
  12.1 0.2 copy-done.1
  12.2 3.4 %fusion.18 = f32[512,8]{0,1:T(8,128)S(1)} fusion(f32[4096,8]{0,1:T(8,128)S(1)} %copy-done, bf16[512,4096]{1,0:T(8,128)(2,1)S(1)} %copy-done.1, f32[4096]{0:T(1024)S(1)} %copy-done.3, f32[512]{0:T(512)S(1)} %add_rsqrt_fusion), kind=kOutput, calls=%fused_computation.16 | convolution fusion | flops 209727488 | bytes 4360192 | tf_op jit(solution)/shard_map/dot_general | solution.py:15
  15.7 0.0 copy-done.2
  15.7 42.8 %all-gather.5.cloned.1.call-done = bf16[2,4096,256]{2,1,0:T(8,128)(2,1)} async-done(((bf16[2,512,256]{2,1,0:T(8,128)(2,1)}), bf16[2,4096,256]{2,1,0:T(8,128)(2,1)}) %all-gather.5.cloned.1.call-update) | async-done | bytes 4194320 | tf_op jit(solution)/shard_map/all_gather | solution.py:24
  58.6 5.8 %fusion.5 = f32[512,2,256]{2,0,1:T(8,128)S(1)} fusion(bf16[2,4096,256]{2,1,0:T(8,128)(2,1)} %all-gather.5.cloned.1.call-done, bf16[512,4096]{1,0:T(8,128)(2,1)} %param.7, f32[4096]{0:T(1024)S(1)} %copy-done.3, f32[512]{0:T(512)S(1)} %add_rsqrt_fusion), kind=kOutput, calls=%fused_computation.7 | convolution fusion | flops 2155872256 | bytes 9455616 | tf_op jit(solution)/shard_map/td,edf->tef/dot_general | solution.py:28
  64.4 41.5 %all-gather.7.cloned.1.call-done = bf16[2,4096,256]{2,1,0:T(8,128)(2,1)} async-done(((bf16[2,512,256]{2,1,0:T(8,128)(2,1)}), bf16[2,4096,256]{2,1,0:T(8,128)(2,1)}) %all-gather.7.cloned.1.call-update) | async-done | bytes 4194320 | tf_op jit(solution)/shard_map/all_gather | solution.py:25
  105.9 6.8 %fusion.13 = bf16[512,2,256]{2,0,1:T(8,128)(2,1)} fusion(bf16[2,4096,256]{2,1,0:T(8,128)(2,1)} %all-gather.7.cloned.1.call-done, f32[512,2,256]{2,0,1:T(8,128)S(1)} %fusion.5, f32[512,2]{0,1:T(2,128)S(1)} %fusion.20, bf16[512,4096]{1,0:T(8,128)(2,1)} %param.7, f32[4096]{0:T(1024)S(1)} %copy-done.3, f32[512]{0:T(512)S(1)} %add_rsqrt_fusion), kind=kOutput, calls=%fused_computation.12 | convolution fusion | flops 2157707264 | bytes 9984000 | tf_op jit(solution)/shard_map/td,edf->tef/dot_general | solution.py:29
  112.6 0.0 all-gather.9.cloned.1.call-update
  112.7 40.5 %all-gather.11.cloned.1.call-done = bf16[2,1024,1024]{2,1,0:T(8,128)(2,1)} async-done(((bf16[2,128,1024]{2,1,0:T(8,128)(2,1)}), bf16[2,1024,1024]{2,1,0:T(8,128)(2,1)}) %all-gather.11.cloned.1.call-update) | async-done | bytes 4194320 | tf_op jit(solution)/shard_map/all_gather | solution.py:26
  153.2 35.6 %all-gather.9.cloned.1.call-done = bf16[512,2,1024]{2,0,1:T(8,128)(2,1)} async-done(((bf16[512,2,256]{2,0,1:T(8,128)(2,1)}), bf16[512,2,1024]{2,0,1:T(8,128)(2,1)}) %all-gather.9.cloned.1.call-update) | async-done | bytes 2097168 | tf_op jit(solution)/shard_map/all_gather | solution.py:31
  188.8 6.1 %bitcast_convert_fusion = bf16[512,1024]{1,0:T(8,128)(2,1)} fusion(bf16[512,2,1024]{2,0,1:T(8,128)(2,1)} %all-gather.9.cloned.1.call-done, bf16[2,1024,1024]{2,1,0:T(8,128)(2,1)} %all-gather.11.cloned.1.call-done), kind=kOutput, calls=%fused_computation.9 | convolution fusion | flops 2148007936 | bytes 7340032 | tf_op jit(solution)/shard_map/tef,efd->td/dot_general | solution.py:32
  (3 shorter events, 0.0 us)
Async XLA Ops:
  6.5 5.5 %copy-start = (f32[4096,8]{0,1:T(8,128)S(1)}, f32[4096,8]{0,1:T(8,128)}, u32[]{:S(2)}) copy-start(f32[4096,8]{0,1:T(8,128)} %param.9) | copy-start | bytes 393220
  6.5 5.5 %copy-start.3 = (f32[4096]{0:T(1024)S(1)}, f32[4096]{0:T(1024)}, u32[]{:S(2)}) copy-start(f32[4096]{0:T(1024)} %param.8) | copy-start | bytes 49156
  6.5 52.0 %all-gather.5.cloned.1.call-start = ((), (), s32[]{:S(2)}) async-start(), calls=%async_computation | async-start | bytes 4718592 | tf_op jit(solution)/shard_map/all_gather | solution.py:24
  7.3 98.6 %all-gather.7.cloned.1.call-start = ((), (), s32[]{:S(2)}) async-start(), calls=%async_computation.1 | async-start | bytes 4718592 | tf_op jit(solution)/shard_map/all_gather | solution.py:25
  8.0 145.2 %all-gather.11.cloned.1.call-start = ((), (), s32[]{:S(2)}) async-start(), calls=%async_computation.3 | async-start | bytes 4718592 | tf_op jit(solution)/shard_map/all_gather | solution.py:26
  8.7 180.0 %all-gather.9.cloned.1.call-start = ((), (), s32[]{:S(2)}) async-start(), calls=%async_computation.2 | async-start | bytes 2621440 | tf_op jit(solution)/shard_map/all_gather | solution.py:31
  8.8 3.5 %copy-start.1 = (bf16[512,4096]{1,0:T(8,128)(2,1)S(1)}, bf16[512,4096]{1,0:T(8,128)(2,1)}, u32[]{:S(2)}) copy-start(bf16[512,4096]{1,0:T(8,128)(2,1)} %param.7) | copy-start | bytes 12582916
  12.0 3.6 %copy-start.2 = (s32[512,2]{0,1:T(2,128)S(1)}, s32[512,2]{0,1:T(2,128)}, u32[]{:S(2)}) copy-start(s32[512,2]{0,1:T(2,128)} %param.10) | copy-start | bytes 12292
Sparse Core Ops, SparseCore 0:
  8.9 49.5 all-gather.4
  60.2 45.6 all-gather.6
  107.5 45.6 all-gather.10
  154.9 33.8 all-gather.8
where the time goes:
time: 202 us; the launch traced here: 201 us
  waiting for transfers between devices  162 us (80%)
  matrix products  22.2 us (11%)
  between operations  13.2 us (7%)
  other arithmetic  3.27 us (2%)
    all_gather x1, waiting for transfers between devices, per_device(): lax.all_gather(w_gate, 'dp', axis=1, tiled=True)  42.8 us
    all_gather x1, waiting for transfers between devices, per_device(): lax.all_gather(w_up, 'dp', axis=1, tiled=True)  41.5 us
    all_gather x1, waiting for transfers between devices, per_device(): lax.all_gather(w_down, 'dp', axis=1, tiled=True)  40.5 us
    all_gather x1, waiting for transfers between devices, per_device(): whole_hidden = lax.all_gather(hidden, 'tp', axis=2, tiled=True)  35.6 us
    dot_general x1, matrix products, per_device(): jnp.einsum('td,edf->tef', normed, full_up, preferred_element_type=jnp.flo...  6.76 us
    dot_general x1, matrix products, per_device(): jnp.einsum('tef,efd->td', whole_hidden, full_down, preferred_element_type...  6.12 us
    dot_general x1, matrix products, per_device(): jnp.einsum('td,edf->tef', normed, full_gate, preferred_element_type=jnp.f...  5.84 us
  transfers between devices with their start and end apart: 4, of which 4 were waited for; matrix products, arithmetic and copies ran while one was open for 10% of the time, Pallas kernels for 0%

commit v1 on v0

--- a/solution.py
+++ b/solution.py
@@ -5,6 +5,18 @@
 
 EPS = 1e-06
 ROUTE_SCALE = 2.5
+
+
+def summed_around(x, axis, dim, term):
+    length, here, rows = (lax.axis_size(axis), lax.axis_index(axis), x.shape[dim])
+    right = [(i, (i + 1) % length) for i in range(length)]
+    current, total = (x, None)
+    for step in range(length):
+        following = lax.ppermute(current, axis, right) if step < length - 1 else None
+        absorb = term(current, (here - step) % length * rows)
+        total = absorb if total is None else total + absorb
+        current = following
+    return total
 
 
 def per_device(tokens, gain, router, routes, w_gate, w_up, w_down):
@@ -28,8 +40,17 @@
     gate_value = jnp.einsum("td,edf->tef", normed, full_gate, preferred_element_type=jnp.float32)
     up_value = jnp.einsum("td,edf->tef", normed, full_up, preferred_element_type=jnp.float32)
     hidden = (jax.nn.silu(gate_value) * up_value * held_weights[:, :, None]).astype(jnp.bfloat16)
-    whole_hidden = lax.all_gather(hidden, "tp", axis=2, tiled=True)
-    mixed = jnp.einsum("tef,efd->td", whole_hidden, full_down, preferred_element_type=jnp.float32)
+    mixed = summed_around(
+        hidden,
+        "tp",
+        2,
+        lambda own_block, at: jnp.einsum(
+            "tef,efd->td",
+            own_block,
+            lax.dynamic_slice_in_dim(full_down, at, own_block.shape[2], axis=1),
+            preferred_element_type=jnp.float32,
+        ),
+    )
     return mixed.astype(jnp.bfloat16)
 
 

time: 202 us -> 179 us (0.89)
  waiting for transfers between devices: 162 us -> 138 us
  starting transfers between devices: 0.12 us -> 3.7 us
    all_gather x1 -> x0, waiting for transfers between devices: 35.6 us -> none  [per_device(): whole_hidden = lax.all_gather(hidden, 'tp', axis=2, tiled=True)]
    ppermute x0 -> x3, waiting for transfers between devices: none -> 25.5 us  [summed_around(): lax.ppermute(current, axis, right)]
    all_gather x1, waiting for transfers between devices: 40.5 us -> 25.8 us  [per_device(): lax.all_gather(w_down, 'dp', axis=1, tiled=True)]
    ppermute x0 -> x3, starting transfers between devices: none -> 3.62 us  [summed_around(): lax.ppermute(current, axis, right)]
    dot_general x1 -> x4, matrix products: 6.12 us -> 5.28 us  [per_device(): jnp.einsum('tef,efd->td', own_block, lax.dynamic_slice_in_dim(full_down,...]
  transfers between devices with their start and end apart: 4 -> 6, of which waited for: 4 -> 5; matrix products, arithmetic and copies ran while one was open for 10% -> 12% of each run, Pallas kernels for 0% -> 0%
where the time goes in v1:
time: 179 us
  waiting for transfers between devices  138 us (77%)
  matrix products  20.5 us (11%)
  between operations  13.2 us (7%)
  starting transfers between devices  3.7 us (2%)
  other arithmetic  3.27 us (2%)
    all_gather x1, waiting for transfers between devices, per_device(): lax.all_gather(w_gate, 'dp', axis=1, tiled=True)  42.9 us
    all_gather x1, waiting for transfers between devices, per_device(): lax.all_gather(w_up, 'dp', axis=1, tiled=True)  41.5 us
    all_gather x1, waiting for transfers between devices, per_device(): lax.all_gather(w_down, 'dp', axis=1, tiled=True)  25.8 us
    ppermute x3, waiting for transfers between devices, summed_around(): lax.ppermute(current, axis, right)  25.5 us
    dot_general x1, matrix products, per_device(): jnp.einsum('td,edf->tef', normed, full_up, preferred_element_type=jnp.flo...  5.95 us
    dot_general x1, matrix products, per_device(): jnp.einsum('td,edf->tef', normed, full_gate, preferred_element_type=jnp.f...  5.84 us
    dot_general x4, matrix products, per_device(): jnp.einsum('tef,efd->td', own_block, lax.dynamic_slice_in_dim(full_down,...  5.28 us
    ppermute x3, starting transfers between devices, summed_around(): lax.ppermute(current, axis, right)  3.62 us
  transfers between devices with their start and end apart: 6, of which 5 were waited for; matrix products, arithmetic and copies ran while one was open for 12% of the time, Pallas kernels for 0%

profile of v1, /device:TPU:0, one launch (start us, length us, event | category | flops | bytes accessed | tf_op | source)
XLA Modules:
  0.0 178.6 jit_solution(3672714353596637995)
XLA Ops:
  6.5 0.0 copy-start
  6.5 0.0 copy-start.4
  6.5 0.0 all-gather.4.cloned.1.call-start
  6.5 0.7 all-gather.4.cloned.1.call-update
  7.3 0.0 all-gather.6.cloned.1.call-start
  7.3 0.7 all-gather.6.cloned.1.call-update
  8.0 0.0 all-gather.8.cloned.1.call-start
  8.1 0.7 all-gather.8.cloned.1.call-update
  8.7 0.0 copy-start.2
  8.8 3.2 %fusion = f32[512]{0:T(512)S(1)} fusion(bf16[512,4096]{1,0:T(8,128)(2,1)} %param.7), kind=kLoop, calls=%fused_computation.2 | loop fusion | flops 6290944 | bytes 4196352 | tf_op jit(solution)/shard_map/reduce_sum | solution.py:24
  12.0 0.0 copy-done
  12.0 0.0 copy-done.4
  12.0 0.2 copy-done.2
  12.2 3.4 %fusion.19 = f32[512,8]{0,1:T(8,128)S(1)} fusion(f32[4096,8]{0,1:T(8,128)S(1)} %copy-done, bf16[512,4096]{1,0:T(8,128)(2,1)S(1)} %copy-done.2, f32[4096]{0:T(1024)S(1)} %copy-done.4, f32[512]{0:T(512)S(1)} %add_rsqrt_fusion), kind=kOutput, calls=%fused_computation.19 | convolution fusion | flops 209727488 | bytes 4360192 | tf_op jit(solution)/shard_map/dot_general | solution.py:27
  15.6 0.0 copy-done.3
  15.7 42.9 %all-gather.4.cloned.1.call-done = bf16[2,4096,256]{2,1,0:T(8,128)(2,1)} async-done(((bf16[2,512,256]{2,1,0:T(8,128)(2,1)}), bf16[2,4096,256]{2,1,0:T(8,128)(2,1)}) %all-gather.4.cloned.1.call-update) | async-done | bytes 4194320 | tf_op jit(solution)/shard_map/all_gather | solution.py:36
  58.6 5.8 %fusion.5 = f32[512,2,256]{2,0,1:T(8,128)S(1)} fusion(bf16[2,4096,256]{2,1,0:T(8,128)(2,1)} %all-gather.4.cloned.1.call-done, bf16[512,4096]{1,0:T(8,128)(2,1)} %param.7, f32[4096]{0:T(1024)S(1)} %copy-done.4, f32[512]{0:T(512)S(1)} %add_rsqrt_fusion), kind=kOutput, calls=%fused_computation.7 | convolution fusion | flops 2155872256 | bytes 9455616 | tf_op jit(solution)/shard_map/td,edf->tef/dot_general | solution.py:40
  64.4 41.5 %all-gather.6.cloned.1.call-done = bf16[2,4096,256]{2,1,0:T(8,128)(2,1)} async-done(((bf16[2,512,256]{2,1,0:T(8,128)(2,1)}), bf16[2,4096,256]{2,1,0:T(8,128)(2,1)}) %all-gather.6.cloned.1.call-update) | async-done | bytes 4194320 | tf_op jit(solution)/shard_map/all_gather | solution.py:37
  105.9 5.9 %fusion.14 = bf16[512,2,256]{2,0,1:T(8,128)(2,1)S(1)} fusion(bf16[2,4096,256]{2,1,0:T(8,128)(2,1)} %all-gather.6.cloned.1.call-done, f32[512,2,256]{2,0,1:T(8,128)S(1)} %fusion.5, f32[512,2]{0,1:T(2,128)S(1)} %fusion.28, bf16[512,4096]{1,0:T(8,128)(2,1)} %param.7, f32[4096]{0:T(1024)S(1)} %copy-done.4, f32[512]{0:T(512)S(1)} %add_rsqrt_fusion), kind=kOutput, calls=%fused_computation.15 | convolution fusion | flops 2157707264 | bytes 9984000 | tf_op jit(solution)/shard_map/td,edf->tef/dot_general | solution.py:41
  111.8 1.5 collective-permute-start
  113.4 13.5 %collective-permute-done = bf16[512,2,256]{2,0,1:T(8,128)(2,1)S(1)} collective-permute-done((bf16[512,2,256]{2,0,1:T(8,128)(2,1)S(1)}, bf16[512,2,256]{2,0,1:T(8,128)(2,1)S(1)}, u32[]{:S(2)}, u32[]{:S(2)}) %collective-permute-start) | collective-permute-done | bytes 524320 | tf_op jit(solution)/shard_map/ppermute | solution.py:15
  126.8 0.6 collective-permute-start.1
  127.4 25.8 %all-gather.8.cloned.1.call-done = bf16[2,1024,1024]{2,1,0:T(8,128)(2,1)} async-done(((bf16[2,128,1024]{2,1,0:T(8,128)(2,1)}), bf16[2,1024,1024]{2,1,0:T(8,128)(2,1)}) %all-gather.8.cloned.1.call-update) | async-done | bytes 4194320 | tf_op jit(solution)/shard_map/all_gather | solution.py:38
  153.2 0.0 copy-start.1
  153.2 2.1 %fusion.25 = f32[512,1024,1]{1,0,2:T(8,128)S(1)} fusion(bf16[512,2,256]{2,0,1:T(8,128)(2,1)S(1)} %fusion.14, bf16[2,1024,1024]{2,1,0:T(8,128)(2,1)} %all-gather.8.cloned.1.call-done, s32[]{:T(128)S(6)} %select_n.32), kind=kOutput, calls=%fused_computation.25 | convolution fusion | flops 536870912 | bytes 3670020 | tf_op jit(solution)/shard_map/tef,efd->td/dot_general | solution.py:47
  155.3 0.0 collective-permute-done.1
  155.3 1.5 collective-permute-start.2
  156.8 0.0 copy-done.1
  156.8 0.7 fusion.23
  157.5 0.7 fusion.21
  158.3 12.0 %collective-permute-done.2 = bf16[512,2,256]{2,0,1:T(8,128)(2,1)S(1)} collective-permute-done((bf16[512,2,256]{2,0,1:T(8,128)(2,1)S(1)}, bf16[512,2,256]{2,0,1:T(8,128)(2,1)S(1)}, u32[]{:S(2)}, u32[]{:S(2)}) %collective-permute-start.2) | collective-permute-done | bytes 524320 | tf_op jit(solution)/shard_map/ppermute | solution.py:15
  170.3 1.7 fusion.7
  (4 shorter events, 0.0 us)
Async XLA Ops:
  6.5 5.5 %copy-start = (f32[4096,8]{0,1:T(8,128)S(1)}, f32[4096,8]{0,1:T(8,128)}, u32[]{:S(2)}) copy-start(f32[4096,8]{0,1:T(8,128)} %param.9) | copy-start | bytes 393220
  6.5 5.5 %copy-start.4 = (f32[4096]{0:T(1024)S(1)}, f32[4096]{0:T(1024)}, u32[]{:S(2)}) copy-start(f32[4096]{0:T(1024)} %param.8) | copy-start | bytes 49156
  6.5 52.0 %all-gather.4.cloned.1.call-start = ((), (), s32[]{:S(2)}) async-start(), calls=%async_computation | async-start | bytes 4718592 | tf_op jit(solution)/shard_map/all_gather | solution.py:36
  7.3 98.6 %all-gather.6.cloned.1.call-start = ((), (), s32[]{:S(2)}) async-start(), calls=%async_computation.1 | async-start | bytes 4718592 | tf_op jit(solution)/shard_map/all_gather | solution.py:37
  8.0 145.2 %all-gather.8.cloned.1.call-start = ((), (), s32[]{:S(2)}) async-start(), calls=%async_computation.2 | async-start | bytes 4718592 | tf_op jit(solution)/shard_map/all_gather | solution.py:38
  8.7 3.5 %copy-start.2 = (bf16[512,4096]{1,0:T(8,128)(2,1)S(1)}, bf16[512,4096]{1,0:T(8,128)(2,1)}, u32[]{:S(2)}) copy-start(bf16[512,4096]{1,0:T(8,128)(2,1)} %param.7) | copy-start | bytes 12582916
  12.0 3.7 %copy-start.3 = (s32[512,2]{0,1:T(2,128)S(1)}, s32[512,2]{0,1:T(2,128)}, u32[]{:S(2)}) copy-start(s32[512,2]{0,1:T(2,128)} %param.10) | copy-start | bytes 12292
  111.8 15.0 %collective-permute-start = (bf16[512,2,256]{2,0,1:T(8,128)(2,1)S(1)}, bf16[512,2,256]{2,0,1:T(8,128)(2,1)S(1)}, u32[]{:S(2)}, u32[]{:S(2)}) collective-permute-start(bf16[512,2,256]{2,0,1:T(8,128)(2,1)S(1)} %fusion.14), channel_id=1, source_target_pairs={{0,1},{1,2},{2,3},{3,0},{4,5},{5,6},{6,7},{7,4},{8,9},{9,10},{10,1... | collective-permute-start | bytes 1572872 | tf_op jit(solution)/shard_map/ppermute | solution.py:15
  126.8 28.4 %collective-permute-start.1 = (bf16[512,2,256]{2,0,1:T(8,128)(2,1)S(1)}, bf16[512,2,256]{2,0,1:T(8,128)(2,1)S(1)}, u32[]{:S(2)}, u32[]{:S(2)}) collective-permute-start(bf16[512,2,256]{2,0,1:T(8,128)(2,1)S(1)} %collective-permute-done), channel_id=1, source_target_pairs={{0,1},{1,2},{2,3},{3,0},{4,5},{5,6},{6,7},{7,4},{8,9},{9,10},{10,1... | collective-permute-start | bytes 1572872 | tf_op jit(solution)/shard_map/ppermute | solution.py:15
  153.2 3.6 %copy-start.1 = (bf16[2,1024,1024]{2,1,0:T(8,128)(2,1)S(1)}, bf16[2,1024,1024]{2,1,0:T(8,128)(2,1)}, u32[]{:S(2)}) copy-start(bf16[2,1024,1024]{2,1,0:T(8,128)(2,1)} %all-gather.8.cloned.1.call-done) | copy-start | bytes 12582916
  155.3 15.0 %collective-permute-start.2 = (bf16[512,2,256]{2,0,1:T(8,128)(2,1)S(1)}, bf16[512,2,256]{2,0,1:T(8,128)(2,1)S(1)}, u32[]{:S(2)}, u32[]{:S(2)}) collective-permute-start(bf16[512,2,256]{2,0,1:T(8,128)(2,1)S(1)} %collective-permute-done.1), channel_id=1, source_target_pairs={{0,1},{1,2},{2,3},{3,0},{4,5},{5,6},{6,7},{7,4},{8,9},{9,10},{10,1... | collective-permute-start | bytes 1572872 | tf_op jit(solution)/shard_map/ppermute | solution.py:15
Sparse Core Ops, SparseCore 0:
  8.9 49.5 all-gather.3
  60.2 45.6 all-gather.5
  107.5 45.6 all-gather.7
